TPU v7x, 128 devices: a whole 4x4x4 slice. The times are simulated.
128 devices in a mesh: gx: 8 (over x, core), gy: 16 (over z, y).
Axes of the slice: x: 4, y: 4, z: 4, core: 2. Of those that a mesh axis runs over, the one named last changes fastest.
Arguments:
- samples: bfloat16 [128, 256, 32, 256], P('gx', 'gy'), may hold values from -6 to 6
- leaf_basis: bfloat16 [64, 256], replicated, may hold values from -0.375 to 0.375
- transfer: bfloat16 [5, 64, 256], replicated, may hold values from -0.5 to 0.5
- coupling: bfloat16 [5, 7, 64, 448], replicated, may hold values from -0.15625 to 0.15625
- near_tiles: bfloat16 [9, 256, 256], replicated, may hold values from -0.125 to 0.125
- codes_local: int32 [128, 256, 4, 27], P('gx', 'gy'), may hold values from 0 to 35, as said below
- counts_local: int32 [128, 256, 4], P('gx', 'gy'), may hold values from 1 to 27, as said below
- codes_upper: int32 [168, 27], replicated, may hold values from 0 to 35, as said below
- counts_upper: int32 [168], replicated, may hold values from 1 to 27, as said below
Outputs:
- response: bfloat16 [128, 256, 32, 256], P('gx', 'gy')
Inputs may be any that keep to these rules, and one draw needn't show every extreme that they name: `codes_local`: entries [i, j, l, :] with i and j multiples of 2^l hold the list of the level-l cluster whose first leaf is (i, j); other entries are not read. Its first count entries are distinct codes a * 6 + b of clusters more than one step away from the target in some direction. `counts_local`: length of the list stored at the same position. `codes_upper`: row n is the list of the n-th cluster of level 4 and coarser, levels in order from 4, row-major within a level, each level with half the rows and columns of the one before and the last with 2 rows; first count entries distinct codes of clusters more than one step away from the target in some direction. `counts_upper`: length of the list of the same row.
All inputs are finite; a program needn't handle non-finite values.
Results may differ from a plain program's by a relative error of at most 0.0095.
Values may be sent and summed in bfloat16 or wider, within the bound.
No kernel may reach another device: no remote copies, remote signals or barrier semaphores. Data moves between devices by JAX's collectives and lax.ppermute only.
A program may use at most 384 MiB of HBM per device.

v0:
```python
import jax
import jax.numpy as jnp
from jax import lax
from jax.sharding import Mesh
from jax.sharding import PartitionSpec as P

GX_GY = ("gx_0", "gx_1", "gy_0", "gy_1")
GX = ("gx_0", "gx_1")
GY = ("gy_0", "gy_1")


def extended(block, sides, width):
    for axis, dim in sides:
        count = lax.axis_size(axis)
        forward = [(i, i + 1) for i in range(count - 1)]
        backward = [(target, source) for source, target in forward]
        low = lax.ppermute(
            lax.slice_in_dim(block, block.shape[dim] - width, None, axis=dim), axis, forward
        )
        high = lax.ppermute(lax.slice_in_dim(block, 0, width, axis=dim), axis, backward)
        block = jnp.concatenate([low, block, high], axis=dim)
    return block


def joined_along(blocks, dim):
    blocks = jnp.moveaxis(blocks, 0, dim)
    lengths = blocks.shape
    return blocks.reshape(*lengths[:dim], lengths[dim] * lengths[dim + 1], *lengths[dim + 2 :])


def stacked_from(value, axes, sequence):
    blocks = value[None]
    for k in sequence:
        blocks = lax.all_gather(blocks, axes[k], axis=0, tiled=True)
    current = [lax.axis_size(axes[k]) for k in reversed(sequence)]
    blocks = blocks.reshape(*current, *value.shape)
    turned = sorted(range(len(sequence)), key=lambda place: sequence[len(sequence) - 1 - place])
    return blocks.transpose(*turned, *range(len(sequence), blocks.ndim)).reshape(-1, *value.shape)


def gathered_by_axis(value, axes, sequence, dim):
    return joined_along(stacked_from(value, axes, sequence), dim)


def is_near(row_step, col_step):
    return abs(row_step) <= 1 and abs(col_step) <= 1


def project(leaf_samples, leaf_basis):
    coeffs = jnp.einsum(
        "ijvs,rs->ijvr", leaf_samples, leaf_basis, preferred_element_type=jnp.float32
    )
    return coeffs.astype(jnp.bfloat16)


def lift_level(children, matrices):
    grid_rows, grid_cols, vectors, rank_size = children.shape
    grouped = children.reshape(grid_rows // 2, 2, grid_cols // 2, 2, vectors, rank_size)
    grouped = grouped.transpose(0, 2, 4, 1, 3, 5).reshape(
        grid_rows // 2, grid_cols // 2, vectors, 4 * rank_size
    )
    parent = jnp.einsum("pqvc,sc->pqvs", grouped, matrices, preferred_element_type=jnp.float32)
    return parent.astype(jnp.bfloat16)


def spread(parent, matrices):
    grid_rows, grid_cols, vectors, rank_size = parent.shape
    carried = jnp.einsum("pqvs,sc->pqvc", parent, matrices, preferred_element_type=jnp.float32)
    carried = carried.reshape(grid_rows, grid_cols, vectors, 2, 2, rank_size).transpose(
        0, 3, 1, 4, 2, 5
    )
    return carried.reshape(2 * grid_rows, 2 * grid_cols, vectors, rank_size)


def member_table(list_codes, counts):
    slot_index = jnp.arange(list_codes.shape[-1], dtype=jnp.int32)
    active = slot_index < counts[..., None]
    matches = (list_codes[..., None] == jnp.arange(36, dtype=jnp.int32)) & active[..., None]
    return jnp.any(matches, axis=-2).astype(jnp.float32)


def couple(padded, member, matrices):
    grid_rows = padded.shape[0] - 4
    grid_cols = padded.shape[1] - 4
    vectors = padded.shape[2]
    rank_size = padded.shape[3]
    member = member.reshape(grid_rows // 2, 2, grid_cols // 2, 2, 36)
    totals = [
        [
            jnp.zeros((grid_rows // 2, grid_cols // 2, vectors, rank_size), jnp.float32)
            for col_bit in range(2)
        ]
        for row_bit in range(2)
    ]
    for code_row in range(6):
        for code_col in range(6):
            parities = [
                (row_bit, col_bit)
                for row_bit in range(2)
                for col_bit in range(2)
                if not is_near(code_row - 2 - row_bit, code_col - 2 - col_bit)
            ]
            if not parities:
                continue
            source = padded[
                code_row : code_row + grid_rows : 2, code_col : code_col + grid_cols : 2
            ]
            blocks = jnp.concatenate(
                [
                    matrices[
                        code_row + 1 - row_bit,
                        :,
                        (code_col + 1 - col_bit) * rank_size : (code_col + 2 - col_bit) * rank_size,
                    ]
                    for row_bit, col_bit in parities
                ],
                axis=0,
            )
            images = jnp.einsum("pqvr,sr->pqvs", source, blocks, preferred_element_type=jnp.float32)
            for number, (row_bit, col_bit) in enumerate(parities):
                weight_mask = member[:, row_bit, :, col_bit, code_row * 6 + code_col]
                totals[row_bit][col_bit] = (
                    totals[row_bit][col_bit]
                    + weight_mask[..., None, None]
                    * images[..., number * rank_size : (number + 1) * rank_size]
                )
    stacked = jnp.stack([jnp.stack(totals[row_bit], axis=0) for row_bit in range(2)], axis=0)
    return stacked.transpose(2, 0, 3, 1, 4, 5).reshape(grid_rows, grid_cols, vectors, rank_size)


def couple_one(padded, member, matrices, row_here, col_here):
    vectors = padded.shape[2]
    rank_size = padded.shape[3]
    window = lax.dynamic_slice(
        padded, (2 * (row_here // 2), 2 * (col_here // 2), 0, 0), (6, 6, vectors, rank_size)
    )
    row_bit = row_here % 2
    col_bit = col_here % 2
    summed = jnp.zeros((vectors, rank_size), jnp.float32)
    for code_row in range(6):
        for code_col in range(6):
            coupling_block = lax.dynamic_slice(
                matrices,
                (code_row + 1 - row_bit, 0, (code_col + 1 - col_bit) * rank_size),
                (1, rank_size, rank_size),
            )[0]
            term = jnp.einsum(
                "vr,sr->vs",
                window[code_row, code_col],
                coupling_block,
                preferred_element_type=jnp.float32,
            )
            summed = summed + member[code_row * 6 + code_col] * term
    return summed


def halo_coeffs(coeffs):
    grid_rows, grid_cols, vectors, rank_size = coeffs.shape
    flattened = coeffs.reshape(grid_rows, grid_cols, vectors * rank_size)
    padded = extended(flattened, ((GX, 0), (GY, 1)), 2)
    return padded.reshape(grid_rows + 4, grid_cols + 4, vectors, rank_size)


def shards(
    samples,
    leaf_basis,
    transfer,
    coupling,
    near_tiles,
    codes_local,
    counts_local,
    codes_upper,
    counts_upper,
):
    patch_size = samples.shape[0]
    vectors = samples.shape[2]
    rank_size = leaf_basis.shape[0]
    levels_local = transfer.shape[0] - 1
    images = []
    wide_samples = extended(samples, ((GX, 0), (GY, 1)), 2)
    first_padded = project(wide_samples, leaf_basis)
    leaf_coeffs = first_padded[2:-2, 2:-2]
    rim_samples = wide_samples[1:-1, 1:-1]
    coeffs = leaf_coeffs
    for level_index in range(levels_local):
        stride = 2**level_index
        member = member_table(
            codes_local[::stride, ::stride, level_index],
            counts_local[::stride, ::stride, level_index],
        )
        if level_index == 0 and first_padded is not None:
            padded = first_padded
        else:
            padded = halo_coeffs(coeffs)
        images.append(couple(padded, member, coupling[level_index]))
        coeffs = lift_level(coeffs, transfer[level_index])
    flat_block = coeffs.reshape(1, vectors * rank_size)
    everything = gathered_by_axis(flat_block, GX_GY, (0, 2, 3, 1), 0)
    block_grid = everything.reshape(lax.axis_size(GX), lax.axis_size(GY), vectors, rank_size)
    upper_coeffs = [block_grid]
    while upper_coeffs[-1].shape[0] > 2:
        upper_coeffs.append(lift_level(upper_coeffs[-1], transfer[levels_local]))
    row_index = lax.axis_index(GX)
    col_index = lax.axis_index(GY)
    offset = 0
    upper_images = []
    for upper_step, coeffs_here in enumerate(upper_coeffs):
        grid_cols = coeffs_here.shape[1]
        row_here = row_index // 2**upper_step
        col_here = col_index // 2**upper_step
        index_here = offset + row_here * grid_cols + col_here
        list_row = lax.dynamic_slice_in_dim(codes_upper, index_here, 1, 0)
        count_row = lax.dynamic_slice_in_dim(counts_upper, index_here, 1, 0)
        member = member_table(list_row, count_row)[0]
        padded = jnp.pad(coeffs_here, ((2, 2), (2, 2), (0, 0), (0, 0)))
        upper_images.append(couple_one(padded, member, coupling[levels_local], row_here, col_here))
        offset = offset + coeffs_here.shape[0] * grid_cols
    downward = upper_images[-1]
    for upper_step in range(len(upper_coeffs) - 2, -1, -1):
        row_here = row_index // 2**upper_step
        col_here = col_index // 2**upper_step
        child_slot = row_here % 2 * 2 + col_here % 2
        carried = jnp.einsum(
            "vs,sc->vc",
            downward.astype(jnp.bfloat16),
            transfer[levels_local],
            preferred_element_type=jnp.float32,
        )
        downward = upper_images[upper_step] + lax.dynamic_slice_in_dim(
            carried, child_slot * rank_size, rank_size, 1
        )
    downward = downward[None, None]
    for level_index in range(levels_local - 1, -1, -1):
        downward = images[level_index] + spread(
            downward.astype(jnp.bfloat16), transfer[level_index]
        )
    summed = jnp.einsum(
        "ijvr,rs->ijvs",
        downward.astype(jnp.bfloat16),
        leaf_basis,
        preferred_element_type=jnp.float32,
    )
    for step_row in range(3):
        for step_col in range(3):
            neighbour = rim_samples[
                step_row : step_row + patch_size, step_col : step_col + patch_size
            ]
            summed = summed + jnp.einsum(
                "ijvs,ts->ijvt",
                neighbour,
                near_tiles[step_row * 3 + step_col],
                preferred_element_type=jnp.float32,
            )
    return summed.astype(jnp.bfloat16)


def solution(mesh):
    torus = Mesh(mesh.devices.reshape(4, 2, 4, 4), ("gx_0", "gx_1", "gy_0", "gy_1"))
    in_specs = (
        P(GX, GY, None, None),
        P(),
        P(),
        P(),
        P(),
        P(GX, GY, None, None),
        P(GX, GY, None),
        P(),
        P(),
    )
    out_specs = P(GX, GY, None, None)
    return jax.shard_map(
        shards, mesh=torus, in_specs=in_specs, out_specs=out_specs, check_vma=False
    )
```

profile of v0, /device:TPU:38, one launch (start us, length us, event | category | flops | bytes accessed | tf_op | source)
XLA Modules:
  0.0 625.4 jit_solution(9527153466392710589)
XLA Ops:
  41.1 5.5 fusion.17
  53.1 3.7 slice_reduce_fusion.104
  60.5 3.7 slice_reduce_fusion.107
  78.8 6.7 %fusion.435 = f32[16,16,32,256]{3,2,1,0:T(8,128)} fusion(bf16[16,16,32,256]{3,2,1,0:T(8,128)(2,1)} %param.9, bf16[9,256,256]{2,1,0:T(8,128)(2,1)} %param.13), kind=kOutput, calls=%fused_computation.926 | convolution fusion | flops 1073741824 | bytes 12713984 | tf_op jit(solution)/shard_map/ijvs,ts->ijvt/dot_general | solution.py:248
  86.9 3.7 slice_reduce_fusion.106
  93.7 4.5 collective-permute-start.3
  100.2 5.4 fusion.10
  105.6 5.4 fusion.6
  111.2 6.2 collective-permute-done.2
  130.1 12.0 %all_gather.12 = bf16[4,1,2048]{2,1,0:T(2,128)(2,1)S(1)} all-gather(bf16[1,1,2048]{2,1,0:T(2,128)(2,1)S(1)} %broadcast_in_dim_reshape.3), channel_id=1, replica_groups=mesh['gx_0'=4,'gx_1'=2,'gy_0'=4,'gy_1'=4] {'gx_0'}, dimensions={0}, use_global_device_ids=true | all-gather | bytes 20480 | tf_op jit(solution)/shard_map/all_gather | solution.py:34
  142.1 13.2 %all_gather.13 = bf16[16,1,2048]{2,1,0:T(2,128)(2,1)S(1)} all-gather(bf16[4,1,2048]{2,1,0:T(2,128)(2,1)S(1)} %all_gather.12), channel_id=1, replica_groups=mesh['gx_0'=4,'gx_1'=2,'gy_0'=4,'gy_1'=4] {'gy_0'}, dimensions={0}, use_global_device_ids=true | all-gather | bytes 81920 | tf_op jit(solution)/shard_map/all_gather | solution.py:34
  155.3 12.3 %all_gather.14 = bf16[64,1,2048]{2,0,1:T(8,128)(2,1)S(1)} all-gather(bf16[16,1,2048]{2,0,1:T(8,128)(2,1)S(1)} %copy.124), channel_id=1, replica_groups=mesh['gx_0'=4,'gx_1'=2,'gy_0'=4,'gy_1'=4] {'gy_1'}, dimensions={0}, use_global_device_ids=true | all-gather | bytes 327680 | tf_op jit(solution)/shard_map/all_gather | solution.py:34
  341.3 15.0 %fusion.148 = f32[1,8,8,32,64]{4,3,2,1,0:T(8,128)} fusion(f32[8,8,32,256]{3,2,1,0:T(8,128)} %fusion.267, f32[8,8,32,256]{3,2,1,0:T(8,128)S(1)} %fusion.269, f32[8,8,32,256]{3,2,1,0:T(8,128)} %fusion.271, f32[8,8,32,256]{3,2,1,0:T(8,128)} %fusion.273, f32[8,8,32,256]{3,2,1,0:T(8,128)} %fusion.275, f32[8,8,32,256]{3,2,1,0:T(8,128)} %fusion.277, ...), kind=kLoop, calls=%fused_computation.411 | loop fusion | flops 6946816 | bytes 14686976 | tf_op jit(solution)/shard_map/stack | solution.py:127
  359.0 8.8 %fusion.175 = f32[1,8,8,32,64]{4,3,2,1,0:T(8,128)} fusion(f32[8,8,32,256]{3,2,1,0:T(8,128)S(1)} %copy-done.18, f32[8,8,32,256]{3,2,1,0:T(8,128)S(1)} %fusion.269, f32[8,8,32,256]{3,2,1,0:T(8,128)S(1)} %copy-done.5, f32[8,8,32,256]{3,2,1,0:T(8,128)S(1)} %copy-done.6, f32[8,8,32,256]{3,2,1,0:T(8,128)S(1)} %copy-done.7, f32[8,8,32,256]{3,2,1,0:T(8,128)S(1)} %copy-done.8, ...), kind=kLoop, calls=%fused_computation.465 | loop fusion | flops 6946816 | bytes 14686976 | tf_op jit(solution)/shard_map/stack | solution.py:127
  368.2 12.3 %fusion.202 = f32[1,8,8,32,64]{4,3,2,1,0:T(8,128)} fusion(f32[8,8,32,256]{3,2,1,0:T(8,128)S(1)} %copy-done.18, f32[8,8,32,256]{3,2,1,0:T(8,128)S(1)} %fusion.269, f32[8,8,32,256]{3,2,1,0:T(8,128)S(1)} %copy-done.5, f32[8,8,32,256]{3,2,1,0:T(8,128)S(1)} %copy-done.6, f32[8,8,32,256]{3,2,1,0:T(8,128)S(1)} %copy-done.7, f32[8,8,32,256]{3,2,1,0:T(8,128)S(1)} %copy-done.8, ...), kind=kLoop, calls=%fused_computation.519 | loop fusion | flops 6946816 | bytes 14686976 | tf_op jit(solution)/shard_map/stack | solution.py:127
  380.8 6.4 %fusion.229 = f32[1,8,8,32,64]{4,3,2,1,0:T(8,128)} fusion(f32[8,8,32,256]{3,2,1,0:T(8,128)S(1)} %copy-done.18, f32[8,8,32,256]{3,2,1,0:T(8,128)S(1)} %fusion.269, f32[8,8,32,256]{3,2,1,0:T(8,128)S(1)} %copy-done.5, f32[8,8,32,256]{3,2,1,0:T(8,128)S(1)} %copy-done.6, f32[8,8,32,256]{3,2,1,0:T(8,128)S(1)} %copy-done.7, f32[8,8,32,256]{3,2,1,0:T(8,128)S(1)} %copy-done.8, ...), kind=kLoop, calls=%fused_computation.573 | loop fusion | flops 6946816 | bytes 14686976 | tf_op jit(solution)/shard_map/stack | solution.py:127
  387.2 4.2 maximum_bitcast_fusion.1
  393.2 6.8 %fusion.25 = f32[16,16,32,256]{3,2,1,0:T(8,128)} fusion(bf16[20,16,32,256]{3,2,1,0:T(8,128)(2,1)} %copy-done.1, bf16[20,2,32,256]{3,2,1,0:T(8,128)(2,1)} %copy-done.28, bf16[9,256,256]{2,1,0:T(8,128)(2,1)} %param.13), kind=kOutput, calls=%fused_computation.138 | convolution fusion | flops 1085538304 | bytes 14417920 | tf_op jit(solution)/shard_map/ijvs,ts->ijvt/dot_general | solution.py:248
  400.0 6.7 %fusion.24 = f32[16,16,32,256]{3,2,1,0:T(8,128)} fusion(bf16[20,16,32,256]{3,2,1,0:T(8,128)(2,1)} %copy-done.1, bf16[20,2,32,256]{3,2,1,0:T(8,128)(2,1)S(1)} %copy-done.29, bf16[9,256,256]{2,1,0:T(8,128)(2,1)} %param.13), kind=kOutput, calls=%fused_computation.137 | convolution fusion | flops 1085538304 | bytes 14417920 | tf_op jit(solution)/shard_map/ijvs,ts->ijvt/dot_general | solution.py:248
  406.7 5.5 fusion.26
  412.2 5.4 fusion.22
  417.5 5.4 fusion.23
  426.7 3.8 collective-permute-start.13
  440.4 3.9 collective-permute-start.14
  447.9 6.0 collective-permute-start.11
  458.5 6.2 collective-permute-start.7
  474.9 17.4 %fusion.1578 = f32[1,1,1,32,64]{4,3,0,2,1:T(8,128)S(1)} fusion(f32[1,1,32,256]{3,2,1,0:T(8,128)S(1)} %convolution_bitcast_fusion.4, f32[1,1,32,256]{3,2,1,0:T(8,128)S(1)} %convolution_bitcast_fusion.5, f32[1,1,32,256]{3,2,1,0:T(8,128)S(1)} %convolution_bitcast_fusion.6, f32[1,1,32,256]{3,2,1,0:T(8,128)S(1)} %convolution_bitcast_fusion.7, ...), kind=kLoop, calls=%fused_computation.2436 | loop fusion | flops 108544 | bytes 229484 | tf_op jit(solution)/shard_map/stack | solution.py:127
  492.3 17.0 %fusion.1605 = f32[1,1,1,32,64]{4,3,0,2,1:T(8,128)S(1)} fusion(f32[1,1,32,256]{3,2,1,0:T(8,128)S(1)} %convolution_bitcast_fusion.4, f32[1,1,32,256]{3,2,1,0:T(8,128)S(1)} %convolution_bitcast_fusion.5, f32[1,1,32,256]{3,2,1,0:T(8,128)S(1)} %convolution_bitcast_fusion.6, f32[1,1,32,256]{3,2,1,0:T(8,128)S(1)} %convolution_bitcast_fusion.7, ...), kind=kLoop, calls=%fused_computation.2490 | loop fusion | flops 108544 | bytes 229484 | tf_op jit(solution)/shard_map/stack | solution.py:127
  509.9 16.7 %fusion.1551 = f32[1,1,1,32,64]{4,3,2,1,0:T(8,128)S(1)} fusion(f32[1,1,32,256]{3,2,1,0:T(8,128)S(1)} %convolution_bitcast_fusion.4, f32[1,1,32,256]{3,2,1,0:T(8,128)S(1)} %convolution_bitcast_fusion.5, f32[1,1,32,256]{3,2,1,0:T(8,128)S(1)} %convolution_bitcast_fusion.6, f32[1,1,32,256]{3,2,1,0:T(8,128)S(1)} %convolution_bitcast_fusion.7, ...), kind=kLoop, calls=%fused_computation.2382 | loop fusion | flops 108544 | bytes 229484 | tf_op jit(solution)/shard_map/stack | solution.py:127
  526.7 17.0 %fusion.1524 = f32[1,1,1,32,64]{4,3,2,1,0:T(8,128)S(1)} fusion(f32[1,1,32,256]{3,2,1,0:T(8,128)S(1)} %convolution_bitcast_fusion.4, f32[1,1,32,256]{3,2,1,0:T(8,128)S(1)} %convolution_bitcast_fusion.5, f32[1,1,32,256]{3,2,1,0:T(8,128)S(1)} %convolution_bitcast_fusion.6, f32[1,1,32,256]{3,2,1,0:T(8,128)S(1)} %convolution_bitcast_fusion.7, ...), kind=kLoop, calls=%fused_computation.2328 | loop fusion | flops 108544 | bytes 229484 | tf_op jit(solution)/shard_map/stack | solution.py:127
  594.2 4.4 fusion.1246
  598.7 26.5 %add_convert_fusion = bf16[16,16,32,256]{3,2,1,0:T(8,128)(2,1)} fusion(f32[16,16,32,256]{3,2,1,0:T(8,128)} %fusion.10, f32[16,16,32,256]{3,2,1,0:T(8,128)} %fusion.24, f32[16,16,32,256]{3,2,1,0:T(8,128)} %fusion.22, f32[16,16,32,256]{3,2,1,0:T(8,128)} %fusion.435, f32[16,16,32,256]{3,2,1,0:T(8,128)} %fusion.25, f32[16,16,32,256]{3,2,1,0:T(8,128)} %fusion.23, ...), kind=kOutput, calls=%fused_computation.36 | convolution fusion | flops 1106509824 | bytes 85721088 | tf_op jit(solution)/shard_map/ijvs,ts->ijvt/dot_general | solution.py:248
  (1179 shorter events, 341.2 us)
Async XLA Ops:
  0.0 117.4 %copy-start = (bf16[64,256]{1,0:T(8,128)(2,1)S(1)}, bf16[64,256]{1,0:T(8,128)(2,1)}, u32[]{:S(2)}) copy-start(bf16[64,256]{1,0:T(8,128)(2,1)} %param.10) | copy-start | bytes 98308
  2.3 88.2 %collective-permute-start = (bf16[2,16,32,256]{3,2,1,0:T(8,128)(2,1)}, bf16[2,16,32,256]{3,2,1,0:T(8,128)(2,1)S(1)}, u32[]{:S(2)}, u32[]{:S(2)}) collective-permute-start(bf16[2,16,32,256]{3,2,1,0:T(8,128)(2,1)} %get-tuple-element.334), channel_id=1, source_target_pairs={{0,16},{16,32},{32,48},{48,64},{64,80},{80,96},{96,112},{1,17},{17... | collective-permute-start | bytes 1572872 | tf_op jit(solution)/shard_map/ppermute | solution.py:17
  4.4 89.2 %collective-permute-start.1 = (bf16[2,16,32,256]{3,2,1,0:T(8,128)(2,1)}, bf16[2,16,32,256]{3,2,1,0:T(8,128)(2,1)S(1)}, u32[]{:S(2)}, u32[]{:S(2)}) collective-permute-start(bf16[2,16,32,256]{3,2,1,0:T(8,128)(2,1)} %get-tuple-element.335), channel_id=1, source_target_pairs={{16,0},{32,16},{48,32},{64,48},{80,64},{96,80},{112,96},{17,1},{33... | collective-permute-start | bytes 1572872 | tf_op jit(solution)/shard_map/ppermute | solution.py:20
  93.7 17.4 %collective-permute-start.3 = (bf16[20,2,32,256]{3,2,1,0:T(8,128)(2,1)S(1)}, bf16[20,2,32,256]{3,2,1,0:T(8,128)(2,1)S(1)}, u32[]{:S(2)}, u32[]{:S(2)}) collective-permute-start(bf16[20,2,32,256]{3,2,1,0:T(8,128)(2,1)S(1)} %get-tuple-element.332), channel_id=1, source_target_pairs={{1,0},{2,1},{3,2},{4,3},{5,4},{6,5},{7,6},{8,7},{9,8},{10,9},{11,1... | collective-permute-start | bytes 1966088 | tf_op jit(solution)/shard_map/ppermute | solution.py:20
  98.2 19.2 %collective-permute-start.2 = (bf16[20,2,32,256]{3,2,1,0:T(8,128)(2,1)S(1)}, bf16[20,2,32,256]{3,2,1,0:T(8,128)(2,1)S(1)}, u32[]{:S(2)}, u32[]{:S(2)}) collective-permute-start(bf16[20,2,32,256]{3,2,1,0:T(8,128)(2,1)S(1)} %get-tuple-element.333), channel_id=1, source_target_pairs={{0,1},{1,2},{2,3},{3,4},{4,5},{5,6},{6,7},{7,8},{8,9},{9,10},{10,1... | collective-permute-start | bytes 1966088 | tf_op jit(solution)/shard_map/ppermute | solution.py:17
  230.5 217.3 %collective-permute-start.4 = (bf16[2,8,2048]{2,1,0:T(8,128)(2,1)}, bf16[2,8,2048]{2,1,0:T(8,128)(2,1)}, u32[]{:S(2)}, u32[]{:S(2)}) collective-permute-start(bf16[2,8,2048]{2,1,0:T(8,128)(2,1)} %slice.5004), channel_id=1, source_target_pairs={{0,16},{16,32},{32,48},{48,64},{64,80},{80,96},{96,112},{1,17},{17... | collective-permute-start | bytes 196616 | tf_op jit(solution)/shard_map/ppermute | solution.py:17
  232.6 200.8 %collective-permute-start.12 = (bf16[2,2,2048]{2,1,0:T(2,128)(2,1)}, bf16[2,2,2048]{2,1,0:T(2,128)(2,1)}, u32[]{:S(2)}, u32[]{:S(2)}) collective-permute-start(bf16[2,2,2048]{2,1,0:T(2,128)(2,1)} %reshape.1625), channel_id=1, source_target_pairs={{0,16},{16,32},{32,48},{48,64},{64,80},{80,96},{96,112},{1,17},{17... | collective-permute-start | bytes 49160 | tf_op jit(solution)/shard_map/ppermute | solution.py:17
  235.2 205.2 %collective-permute-start.8 = (bf16[2,4,2048]{2,1,0:T(4,128)(2,1)}, bf16[2,4,2048]{2,1,0:T(4,128)(2,1)}, u32[]{:S(2)}, u32[]{:S(2)}) collective-permute-start(bf16[2,4,2048]{2,1,0:T(4,128)(2,1)} %slice.5302), channel_id=1, source_target_pairs={{0,16},{16,32},{32,48},{48,64},{64,80},{80,96},{96,112},{1,17},{17... | collective-permute-start | bytes 98312 | tf_op jit(solution)/shard_map/ppermute | solution.py:17
  426.7 11.7 %collective-permute-start.13 = (bf16[2,2,2048]{2,1,0:T(2,128)(2,1)}, bf16[2,2,2048]{2,1,0:T(2,128)(2,1)S(1)}, u32[]{:S(2)}, u32[]{:S(2)}) collective-permute-start(bf16[2,2,2048]{2,1,0:T(2,128)(2,1)} %reshape.1625), channel_id=1, source_target_pairs={{16,0},{32,16},{48,32},{64,48},{80,64},{96,80},{112,96},{17,1},{33... | collective-permute-start | bytes 49160 | tf_op jit(solution)/shard_map/ppermute | solution.py:20
  430.8 24.1 %collective-permute-start.5 = (bf16[2,8,2048]{2,1,0:T(8,128)(2,1)S(1)}, bf16[2,8,2048]{2,1,0:T(8,128)(2,1)S(1)}, u32[]{:S(2)}, u32[]{:S(2)}) collective-permute-start(bf16[2,8,2048]{2,1,0:T(8,128)(2,1)S(1)} %slice.5006), channel_id=1, source_target_pairs={{16,0},{32,16},{48,32},{64,48},{80,64},{96,80},{112,96},{17,1},{33... | collective-permute-start | bytes 196616 | tf_op jit(solution)/shard_map/ppermute | solution.py:20
  433.4 11.7 %collective-permute-start.9 = (bf16[2,4,2048]{2,1,0:T(4,128)(2,1)S(1)}, bf16[2,4,2048]{2,1,0:T(4,128)(2,1)S(1)}, u32[]{:S(2)}, u32[]{:S(2)}) collective-permute-start(bf16[2,4,2048]{2,1,0:T(4,128)(2,1)S(1)} %slice.5304), channel_id=1, source_target_pairs={{16,0},{32,16},{48,32},{64,48},{80,64},{96,80},{112,96},{17,1},{33... | collective-permute-start | bytes 98312 | tf_op jit(solution)/shard_map/ppermute | solution.py:20
  438.5 20.0 %collective-permute-start.15 = (bf16[6,2,2048]{2,1,0:T(2,128)(2,1)S(1)}, bf16[6,2,2048]{2,1,0:T(2,128)(2,1)S(1)}, u32[]{:S(2)}, u32[]{:S(2)}) collective-permute-start(bf16[6,2,2048]{2,1,0:T(2,128)(2,1)S(1)} %constant_dynamic-update-slice_fusion.9), channel_id=1, source_target_pairs={{1,0},{2,1},{3,2},{4,3},{5,4},{6,5},{7,6},{8,7},{9,8},{10,9},{11,1... | collective-permute-start | bytes 147464 | tf_op jit(solution)/shard_map/ppermute | solution.py:20
  440.4 24.3 %collective-permute-start.14 = (bf16[6,2,2048]{2,1,0:T(2,128)(2,1)S(1)}, bf16[6,2,2048]{2,1,0:T(2,128)(2,1)S(1)}, u32[]{:S(2)}, u32[]{:S(2)}) collective-permute-start(bf16[6,2,2048]{2,1,0:T(2,128)(2,1)S(1)} %constant_dynamic-update-slice_fusion.9), channel_id=1, source_target_pairs={{0,1},{1,2},{2,3},{3,4},{4,5},{5,6},{6,7},{7,8},{8,9},{9,10},{10,1... | collective-permute-start | bytes 147464 | tf_op jit(solution)/shard_map/ppermute | solution.py:17
  446.0 98.3 %collective-permute-start.10 = (bf16[8,2,2048]{2,1,0:T(2,128)(2,1)}, bf16[8,2,2048]{2,1,0:T(2,128)(2,1)}, u32[]{:S(2)}, u32[]{:S(2)}) collective-permute-start(bf16[8,2,2048]{2,1,0:T(2,128)(2,1)} %get-tuple-element.509), channel_id=1, source_target_pairs={{0,1},{1,2},{2,3},{3,4},{4,5},{5,6},{6,7},{7,8},{8,9},{9,10},{10,1... | collective-permute-start | bytes 196616 | tf_op jit(solution)/shard_map/ppermute | solution.py:17
  447.9 96.4 %collective-permute-start.11 = (bf16[8,2,2048]{2,1,0:T(2,128)(2,1)}, bf16[8,2,2048]{2,1,0:T(2,128)(2,1)}, u32[]{:S(2)}, u32[]{:S(2)}) collective-permute-start(bf16[8,2,2048]{2,1,0:T(2,128)(2,1)} %get-tuple-element.510), channel_id=1, source_target_pairs={{1,0},{2,1},{3,2},{4,3},{5,4},{6,5},{7,6},{8,7},{9,8},{10,9},{11,1... | collective-permute-start | bytes 196616 | tf_op jit(solution)/shard_map/ppermute | solution.py:20
  456.5 106.2 %collective-permute-start.6 = (bf16[12,2,2048]{2,1,0:T(2,128)(2,1)}, bf16[12,2,2048]{2,1,0:T(2,128)(2,1)}, u32[]{:S(2)}, u32[]{:S(2)}) collective-permute-start(bf16[12,2,2048]{2,1,0:T(2,128)(2,1)} %get-tuple-element.503), channel_id=1, source_target_pairs={{0,1},{1,2},{2,3},{3,4},{4,5},{5,6},{6,7},{7,8},{8,9},{9,10},{10,1... | collective-permute-start | bytes 294920 | tf_op jit(solution)/shard_map/ppermute | solution.py:17
  458.5 104.1 %collective-permute-start.7 = (bf16[12,2,2048]{2,1,0:T(2,128)(2,1)}, bf16[12,2,2048]{2,1,0:T(2,128)(2,1)}, u32[]{:S(2)}, u32[]{:S(2)}) collective-permute-start(bf16[12,2,2048]{2,1,0:T(2,128)(2,1)} %get-tuple-element.504), channel_id=1, source_target_pairs={{1,0},{2,1},{3,2},{4,3},{5,4},{6,5},{7,6},{8,7},{9,8},{10,9},{11,1... | collective-permute-start | bytes 294920 | tf_op jit(solution)/shard_map/ppermute | solution.py:20
  474.5 71.5 %copy-start.67 = (bf16[64,64]{0,1:T(8,128)(2,1)S(1)}, bf16[64,64]{0,1:T(8,128)(2,1)}, u32[]{:S(2)}) copy-start(bf16[64,64]{0,1:T(8,128)(2,1)} %get-tuple-element.414) | copy-start | bytes 24580
  474.5 71.5 %copy-start.68 = (bf16[64,64]{0,1:T(8,128)(2,1)S(1)}, bf16[64,64]{0,1:T(8,128)(2,1)}, u32[]{:S(2)}) copy-start(bf16[64,64]{0,1:T(8,128)(2,1)} %get-tuple-element.416) | copy-start | bytes 24580
  474.7 71.5 %copy-start.69 = (bf16[64,64]{0,1:T(8,128)(2,1)S(1)}, bf16[64,64]{0,1:T(8,128)(2,1)}, u32[]{:S(2)}) copy-start(bf16[64,64]{0,1:T(8,128)(2,1)} %get-tuple-element.418) | copy-start | bytes 24580
  474.7 71.7 %copy-start.73 = (bf16[64,64]{0,1:T(8,128)(2,1)S(1)}, bf16[64,64]{0,1:T(8,128)(2,1)}, u32[]{:S(2)}) copy-start(bf16[64,64]{0,1:T(8,128)(2,1)} %get-tuple-element.404) | copy-start | bytes 24580
  474.7 71.7 %copy-start.76 = (bf16[64,64]{0,1:T(8,128)(2,1)S(1)}, bf16[64,64]{0,1:T(8,128)(2,1)}, u32[]{:S(2)}) copy-start(bf16[64,64]{0,1:T(8,128)(2,1)} %get-tuple-element.399) | copy-start | bytes 24580
  474.8 71.8 %copy-start.71 = (bf16[64,64]{0,1:T(8,128)(2,1)S(1)}, bf16[64,64]{0,1:T(8,128)(2,1)}, u32[]{:S(2)}) copy-start(bf16[64,64]{0,1:T(8,128)(2,1)} %get-tuple-element.408) | copy-start | bytes 24580
  474.8 72.0 %copy-start.78 = (bf16[64,64]{0,1:T(8,128)(2,1)S(1)}, bf16[64,64]{0,1:T(8,128)(2,1)}, u32[]{:S(2)}) copy-start(bf16[64,64]{0,1:T(8,128)(2,1)} %get-tuple-element.392) | copy-start | bytes 24580
  474.8 72.0 %copy-start.79 = (bf16[64,64]{0,1:T(8,128)(2,1)S(1)}, bf16[64,64]{0,1:T(8,128)(2,1)}, u32[]{:S(2)}) copy-start(bf16[64,64]{0,1:T(8,128)(2,1)} %get-tuple-element.391) | copy-start | bytes 24580
  474.8 72.2 %copy-start.77 = (bf16[64,64]{0,1:T(8,128)(2,1)S(1)}, bf16[64,64]{0,1:T(8,128)(2,1)}, u32[]{:S(2)}) copy-start(bf16[64,64]{0,1:T(8,128)(2,1)} %get-tuple-element.393) | copy-start | bytes 24580
  492.2 55.0 %copy-start.66 = (bf16[64,64]{0,1:T(8,128)(2,1)S(1)}, bf16[64,64]{0,1:T(8,128)(2,1)}, u32[]{:S(2)}) copy-start(bf16[64,64]{0,1:T(8,128)(2,1)} %get-tuple-element.402) | copy-start | bytes 24580
  492.2 55.0 %copy-start.74 = (bf16[64,64]{0,1:T(8,128)(2,1)S(1)}, bf16[64,64]{0,1:T(8,128)(2,1)}, u32[]{:S(2)}) copy-start(bf16[64,64]{0,1:T(8,128)(2,1)} %get-tuple-element.397) | copy-start | bytes 24580
  492.2 55.2 %copy-start.65 = (bf16[64,64]{0,1:T(8,128)(2,1)S(1)}, bf16[64,64]{0,1:T(8,128)(2,1)}, u32[]{:S(2)}) copy-start(bf16[64,64]{0,1:T(8,128)(2,1)} %get-tuple-element.406) | copy-start | bytes 24580
  492.3 55.5 %copy-start.59 = (bf16[64,64]{0,1:T(8,128)(2,1)S(1)}, bf16[64,64]{0,1:T(8,128)(2,1)}, u32[]{:S(2)}) copy-start(bf16[64,64]{0,1:T(8,128)(2,1)} %get-tuple-element.390) | copy-start | bytes 24580
  492.3 55.7 %copy-start.130 = (bf16[64,64]{0,1:T(8,128)(2,1)S(1)}, bf16[64,64]{0,1:T(8,128)(2,1)}, u32[]{:S(2)}) copy-start(bf16[64,64]{0,1:T(8,128)(2,1)} %get-tuple-element.383) | copy-start | bytes 24580
  492.3 55.7 %copy-start.136 = (bf16[64,64]{0,1:T(8,128)(2,1)S(1)}, bf16[64,64]{0,1:T(8,128)(2,1)}, u32[]{:S(2)}) copy-start(bf16[64,64]{0,1:T(8,128)(2,1)} %get-tuple-element.384) | copy-start | bytes 24580
  (364 other events, 2996.3 us)
where the time goes:
time: 637 us; the launch traced here: 625 us
  matrix products  268 us (42%)
  other arithmetic  143 us (22%)
  local copies, waits for them, and re-layouts  112 us (18%)
  starting transfers between devices  49.8 us (8%)
  blocking collectives  39.7 us (6%)
  between operations  6.47 us (1%)
  waiting for transfers between devices  6.44 us (1%)
    another operation x16, other arithmetic, couple(): jnp.stack(totals[row_bit], axis=0)  125 us
    dot_general x106, matrix products, couple_one(): jnp.einsum('vr,sr->vs', window[code_row, code_col], coupling_block, prefe...  92.1 us
    dot_general x128, matrix products, couple(): jnp.einsum('pqvr,sr->pqvs', source, blocks, preferred_element_type=jnp.fl...  86.4 us
    dot_general x9, matrix products, shards(): jnp.einsum('ijvs,ts->ijvt', neighbour, near_tiles[step_row * 3 + step_col...  73.8 us
    all_gather x4, blocking collectives, stacked_from(): blocks = lax.all_gather(blocks, axes[k], axis=0, tiled=True)  39.7 us
    slice x24, local copies, waits for them, and re-layouts, couple(): weight_mask = member[:, row_bit, :, col_bit, code_row * 6 + code_col]  39.4 us
    ppermute x8, starting transfers between devices, extended(): lax.ppermute(lax.slice_in_dim(block, 0, width, axis=dim), axis, backward)  32.1 us
    ppermute x8, starting transfers between devices, extended(): lax.ppermute(lax.slice_in_dim(block, block.shape[dim] - width, None, axis...  17.7 us
  transfers between devices with their start and end apart: 16, of which 2 were waited for; matrix products, arithmetic and copies ran while one was open for 61% of the time, Pallas kernels for 0%

commit v1 on v0

--- a/solution.py
+++ b/solution.py
@@ -3,10 +3,17 @@
 from jax import lax
 from jax.sharding import Mesh
 from jax.sharding import PartitionSpec as P
+from jax.lax import all_to_all, psum
 
 GX_GY = ("gx_0", "gx_1", "gy_0", "gy_1")
 GX = ("gx_0", "gx_1")
 GY = ("gy_0", "gy_1")
+
+
+def load_heaps_over_axis(u, mesh_name):
+    return jnp.concatenate(
+        all_to_all(jnp.stack([u] * psum(1, mesh_name), axis=0), mesh_name, 0, 0), axis=0
+    )
 
 
 def extended(block, sides, width):
@@ -31,7 +38,7 @@
 def stacked_from(value, axes, sequence):
     blocks = value[None]
     for k in sequence:
-        blocks = lax.all_gather(blocks, axes[k], axis=0, tiled=True)
+        blocks = load_heaps_over_axis(blocks, axes[k])
     current = [lax.axis_size(axes[k]) for k in reversed(sequence)]
     blocks = blocks.reshape(*current, *value.shape)
     turned = sorted(range(len(sequence)), key=lambda place: sequence[len(sequence) - 1 - place])

time: 637 us -> 587 us (0.922)
  blocking collectives: 39.7 us -> 4.15 us
  matrix products: 268 us -> 252 us
  starting transfers between devices: 49.8 us -> 65.3 us
  local copies, waits for them, and re-layouts: 112 us -> 105 us
    all_gather x4 -> x0, blocking collectives: 39.7 us -> none  [stacked_from(): blocks = lax.all_gather(blocks, axes[k], axis=0, tiled=True)]
    all_to_all x0 -> x3, starting transfers between devices: none -> 18.1 us  [load_heaps_over_axis(): all_to_all(jnp.stack([u] * psum(1, mesh_name), axis=0), mesh_name, 0, 0)]
    dot_general x128, matrix products: 86.4 us -> 72.9 us  [couple(): jnp.einsum('pqvr,sr->pqvs', source, blocks, preferred_element_type=jnp.fl...]
    unnamed x769 -> x718, local copies, waits for them, and re-layouts: 15.3 us -> 12.8 us
  transfers between devices with their start and end apart: 16 -> 19, of which waited for: 2 -> 2; matrix products, arithmetic and copies ran while one was open for 61% -> 49% of each run, Pallas kernels for 0% -> 0%
where the time goes in v1:
time: 587 us; the launch traced here: 576 us
  matrix products  252 us (43%)
  other arithmetic  138 us (24%)
  local copies, waits for them, and re-layouts  105 us (18%)
  starting transfers between devices  65.3 us (11%)
  between operations  6.61 us (1%)
  waiting for transfers between devices  6.46 us (1%)
    another operation x16, other arithmetic, couple(): jnp.stack(totals[row_bit], axis=0)  124 us
    dot_general x106, matrix products, couple_one(): jnp.einsum('vr,sr->vs', window[code_row, code_col], coupling_block, prefe...  88.8 us
    dot_general x128, matrix products, couple(): jnp.einsum('pqvr,sr->pqvs', source, blocks, preferred_element_type=jnp.fl...  72.9 us
    dot_general x9, matrix products, shards(): jnp.einsum('ijvs,ts->ijvt', neighbour, near_tiles[step_row * 3 + step_col...  71.4 us
    slice x24, local copies, waits for them, and re-layouts, couple(): weight_mask = member[:, row_bit, :, col_bit, code_row * 6 + code_col]  39.4 us
    ppermute x8, starting transfers between devices, extended(): lax.ppermute(lax.slice_in_dim(block, 0, width, axis=dim), axis, backward)  29.6 us
    all_to_all x3, starting transfers between devices, load_heaps_over_axis(): all_to_all(jnp.stack([u] * psum(1, mesh_name), axis=0), mesh_name, 0, 0)  18.1 us
    ppermute x8, starting transfers between devices, extended(): lax.ppermute(lax.slice_in_dim(block, block.shape[dim] - width, None, axis...  17.6 us
  transfers between devices with their start and end apart: 19, of which 2 were waited for; matrix products, arithmetic and copies ran while one was open for 49% of the time, Pallas kernels for 0%

profile of v1, /device:TPU:38, one launch (start us, length us, event | category | flops | bytes accessed | tf_op | source)
XLA Modules:
  0.0 576.3 jit_solution(12899410287417693661)
XLA Ops:
  41.9 3.7 slice_reduce_fusion.103
  45.6 3.7 slice_reduce_fusion.104
  53.0 3.7 slice_reduce_fusion.107
  70.9 6.7 %fusion.435 = f32[16,16,32,256]{3,2,1,0:T(8,128)} fusion(bf16[16,16,32,256]{3,2,1,0:T(8,128)(2,1)} %param.9, bf16[9,256,256]{2,1,0:T(8,128)(2,1)} %param.13), kind=kOutput, calls=%fused_computation.928 | convolution fusion | flops 1073741824 | bytes 12713984 | tf_op jit(solution)/shard_map/ijvs,ts->ijvt/dot_general | solution.py:255
  79.0 3.7 slice_reduce_fusion.106
  85.9 4.5 collective-permute-start.3
  92.3 5.4 fusion.10
  97.7 5.4 fusion.6
  103.3 6.2 %collective-permute-done.2 = bf16[20,2,32,256]{3,2,1,0:T(8,128)(2,1)S(1)} collective-permute-done((bf16[20,2,32,256]{3,2,1,0:T(8,128)(2,1)S(1)}, bf16[20,2,32,256]{3,2,1,0:T(8,128)(2,1)S(1)}, u32[]{:S(2)}, u32[]{:S(2)}) %collective-permute-start.2) | collective-permute-done | bytes 655392 | tf_op jit(solution)/shard_map/ppermute | solution.py:24
  168.9 5.4 reshape.1625
  190.4 6.9 %all-to-all-start = ((bf16[4,2,1024]{2,1,0:T(2,128)(2,1)}), bf16[4,2,1024]{2,1,0:T(2,128)(2,1)S(1)}, u32[]{:S(2)}, u32[]{:S(2)}) async-start(bf16[4,2,1024]{2,1,0:T(2,128)(2,1)} %reshape.2124), calls=%async_computation | async-start | bytes 32768 | tf_op jit(solution)/shard_map/all_to_all | solution.py:15
  201.2 15.0 %fusion.148 = f32[1,8,8,32,64]{4,3,2,1,0:T(8,128)} fusion(f32[8,8,32,256]{3,2,1,0:T(8,128)} %fusion.267, f32[8,8,32,256]{3,2,1,0:T(8,128)S(1)} %fusion.269, f32[8,8,32,256]{3,2,1,0:T(8,128)} %fusion.271, f32[8,8,32,256]{3,2,1,0:T(8,128)} %fusion.273, f32[8,8,32,256]{3,2,1,0:T(8,128)} %fusion.275, f32[8,8,32,256]{3,2,1,0:T(8,128)} %fusion.277, ...), kind=kLoop, calls=%fused_computation.411 | loop fusion | flops 6946816 | bytes 14686976 | tf_op jit(solution)/shard_map/stack | solution.py:134
  218.9 8.2 %fusion.175 = f32[1,8,8,32,64]{4,3,2,1,0:T(8,128)} fusion(f32[8,8,32,256]{3,2,1,0:T(8,128)S(1)} %copy-done.16, f32[8,8,32,256]{3,2,1,0:T(8,128)S(1)} %fusion.269, f32[8,8,32,256]{3,2,1,0:T(8,128)S(1)} %copy-done.3, f32[8,8,32,256]{3,2,1,0:T(8,128)S(1)} %copy-done.4, f32[8,8,32,256]{3,2,1,0:T(8,128)S(1)} %copy-done.5, f32[8,8,32,256]{3,2,1,0:T(8,128)S(1)} %copy-done.6, ...), kind=kLoop, calls=%fused_computation.465 | loop fusion | flops 6946816 | bytes 14686976 | tf_op jit(solution)/shard_map/stack | solution.py:134
  227.4 12.3 %fusion.202 = f32[1,8,8,32,64]{4,3,2,1,0:T(8,128)} fusion(f32[8,8,32,256]{3,2,1,0:T(8,128)S(1)} %copy-done.16, f32[8,8,32,256]{3,2,1,0:T(8,128)S(1)} %fusion.269, f32[8,8,32,256]{3,2,1,0:T(8,128)S(1)} %copy-done.3, f32[8,8,32,256]{3,2,1,0:T(8,128)S(1)} %copy-done.4, f32[8,8,32,256]{3,2,1,0:T(8,128)S(1)} %copy-done.5, f32[8,8,32,256]{3,2,1,0:T(8,128)S(1)} %copy-done.6, ...), kind=kLoop, calls=%fused_computation.519 | loop fusion | flops 6946816 | bytes 14686976 | tf_op jit(solution)/shard_map/stack | solution.py:134
  240.0 7.4 %fusion.229 = f32[1,8,8,32,64]{4,3,2,1,0:T(8,128)} fusion(f32[8,8,32,256]{3,2,1,0:T(8,128)S(1)} %copy-done.16, f32[8,8,32,256]{3,2,1,0:T(8,128)S(1)} %fusion.269, f32[8,8,32,256]{3,2,1,0:T(8,128)S(1)} %copy-done.3, f32[8,8,32,256]{3,2,1,0:T(8,128)S(1)} %copy-done.4, f32[8,8,32,256]{3,2,1,0:T(8,128)S(1)} %copy-done.5, f32[8,8,32,256]{3,2,1,0:T(8,128)S(1)} %copy-done.6, ...), kind=kLoop, calls=%fused_computation.573 | loop fusion | flops 6946816 | bytes 14686976 | tf_op jit(solution)/shard_map/stack | solution.py:134
  247.5 5.5 fusion.25
  253.0 5.4 fusion.24
  258.4 5.5 fusion.26
  263.9 5.4 fusion.22
  269.2 5.6 fusion.23
  284.8 5.7 all-to-all-start.1
  296.4 3.9 collective-permute-start.14
  304.0 5.5 all-to-all-start.2
  309.5 5.3 collective-permute-start.11
  318.6 6.2 %collective-permute-start.7 = (bf16[12,2,2048]{2,1,0:T(2,128)(2,1)}, bf16[12,2,2048]{2,1,0:T(2,128)(2,1)}, u32[]{:S(2)}, u32[]{:S(2)}) collective-permute-start(bf16[12,2,2048]{2,1,0:T(2,128)(2,1)} %get-tuple-element.504), channel_id=1, source_target_pairs={{1,0},{2,1},{3,2},{4,3},{5,4},{6,5},{7,6},{8,7},{9,8},{10,9},{11,1... | collective-permute-start | bytes 294920 | tf_op jit(solution)/shard_map/ppermute | solution.py:27
  330.6 16.5 %fusion.1578 = f32[1,1,1,32,64]{4,3,0,2,1:T(8,128)S(1)} fusion(f32[1,1,32,256]{3,2,1,0:T(8,128)S(1)} %convolution_bitcast_fusion.4, f32[1,1,32,256]{3,2,1,0:T(8,128)S(1)} %convolution_bitcast_fusion.5, f32[1,1,32,256]{3,2,1,0:T(8,128)S(1)} %convolution_bitcast_fusion.6, f32[1,1,32,256]{3,2,1,0:T(8,128)S(1)} %convolution_bitcast_fusion.7, ...), kind=kLoop, calls=%fused_computation.2438 | loop fusion | flops 108544 | bytes 229484 | tf_op jit(solution)/shard_map/stack | solution.py:134
  347.1 17.1 %fusion.1605 = f32[1,1,1,32,64]{4,3,0,2,1:T(8,128)S(1)} fusion(f32[1,1,32,256]{3,2,1,0:T(8,128)S(1)} %convolution_bitcast_fusion.4, f32[1,1,32,256]{3,2,1,0:T(8,128)S(1)} %convolution_bitcast_fusion.5, f32[1,1,32,256]{3,2,1,0:T(8,128)S(1)} %convolution_bitcast_fusion.6, f32[1,1,32,256]{3,2,1,0:T(8,128)S(1)} %convolution_bitcast_fusion.7, ...), kind=kLoop, calls=%fused_computation.2492 | loop fusion | flops 108544 | bytes 229484 | tf_op jit(solution)/shard_map/stack | solution.py:134
  364.8 17.1 %fusion.1551 = f32[1,1,1,32,64]{4,3,2,1,0:T(8,128)S(1)} fusion(f32[1,1,32,256]{3,2,1,0:T(8,128)S(1)} %convolution_bitcast_fusion.4, f32[1,1,32,256]{3,2,1,0:T(8,128)S(1)} %convolution_bitcast_fusion.5, f32[1,1,32,256]{3,2,1,0:T(8,128)S(1)} %convolution_bitcast_fusion.6, f32[1,1,32,256]{3,2,1,0:T(8,128)S(1)} %convolution_bitcast_fusion.7, ...), kind=kLoop, calls=%fused_computation.2384 | loop fusion | flops 108544 | bytes 229484 | tf_op jit(solution)/shard_map/stack | solution.py:134
  381.9 16.9 %fusion.1524 = f32[1,1,1,32,64]{4,3,2,1,0:T(8,128)S(1)} fusion(f32[1,1,32,256]{3,2,1,0:T(8,128)S(1)} %convolution_bitcast_fusion.4, f32[1,1,32,256]{3,2,1,0:T(8,128)S(1)} %convolution_bitcast_fusion.5, f32[1,1,32,256]{3,2,1,0:T(8,128)S(1)} %convolution_bitcast_fusion.6, f32[1,1,32,256]{3,2,1,0:T(8,128)S(1)} %convolution_bitcast_fusion.7, ...), kind=kLoop, calls=%fused_computation.2330 | loop fusion | flops 108544 | bytes 229484 | tf_op jit(solution)/shard_map/stack | solution.py:134
  436.9 4.2 all_to_all.20
  545.0 4.4 fusion.1246
  549.4 26.5 %add_convert_fusion = bf16[16,16,32,256]{3,2,1,0:T(8,128)(2,1)} fusion(f32[16,16,32,256]{3,2,1,0:T(8,128)} %fusion.10, f32[16,16,32,256]{3,2,1,0:T(8,128)} %fusion.24, f32[16,16,32,256]{3,2,1,0:T(8,128)} %fusion.22, f32[16,16,32,256]{3,2,1,0:T(8,128)} %fusion.435, f32[16,16,32,256]{3,2,1,0:T(8,128)} %fusion.25, f32[16,16,32,256]{3,2,1,0:T(8,128)} %fusion.23, ...), kind=kOutput, calls=%fused_computation.36 | convolution fusion | flops 1106509824 | bytes 85721088 | tf_op jit(solution)/shard_map/ijvs,ts->ijvt/dot_general | solution.py:255
  (1138 shorter events, 314.8 us)
Async XLA Ops:
  0.0 109.5 %copy-start = (bf16[64,256]{1,0:T(8,128)(2,1)S(1)}, bf16[64,256]{1,0:T(8,128)(2,1)}, u32[]{:S(2)}) copy-start(bf16[64,256]{1,0:T(8,128)(2,1)} %param.10) | copy-start | bytes 98308
  2.4 80.3 %collective-permute-start = (bf16[2,16,32,256]{3,2,1,0:T(8,128)(2,1)}, bf16[2,16,32,256]{3,2,1,0:T(8,128)(2,1)S(1)}, u32[]{:S(2)}, u32[]{:S(2)}) collective-permute-start(bf16[2,16,32,256]{3,2,1,0:T(8,128)(2,1)} %get-tuple-element.334), channel_id=1, source_target_pairs={{0,16},{16,32},{32,48},{48,64},{64,80},{80,96},{96,112},{1,17},{17... | collective-permute-start | bytes 1572872 | tf_op jit(solution)/shard_map/ppermute | solution.py:24
  4.4 81.2 %collective-permute-start.1 = (bf16[2,16,32,256]{3,2,1,0:T(8,128)(2,1)}, bf16[2,16,32,256]{3,2,1,0:T(8,128)(2,1)S(1)}, u32[]{:S(2)}, u32[]{:S(2)}) collective-permute-start(bf16[2,16,32,256]{3,2,1,0:T(8,128)(2,1)} %get-tuple-element.335), channel_id=1, source_target_pairs={{16,0},{32,16},{48,32},{64,48},{80,64},{96,80},{112,96},{17,1},{33... | collective-permute-start | bytes 1572872 | tf_op jit(solution)/shard_map/ppermute | solution.py:27
  85.9 17.4 %collective-permute-start.3 = (bf16[20,2,32,256]{3,2,1,0:T(8,128)(2,1)S(1)}, bf16[20,2,32,256]{3,2,1,0:T(8,128)(2,1)S(1)}, u32[]{:S(2)}, u32[]{:S(2)}) collective-permute-start(bf16[20,2,32,256]{3,2,1,0:T(8,128)(2,1)S(1)} %get-tuple-element.332), channel_id=1, source_target_pairs={{1,0},{2,1},{3,2},{4,3},{5,4},{6,5},{7,6},{8,7},{9,8},{10,9},{11,1... | collective-permute-start | bytes 1966088 | tf_op jit(solution)/shard_map/ppermute | solution.py:27
  90.3 19.2 %collective-permute-start.2 = (bf16[20,2,32,256]{3,2,1,0:T(8,128)(2,1)S(1)}, bf16[20,2,32,256]{3,2,1,0:T(8,128)(2,1)S(1)}, u32[]{:S(2)}, u32[]{:S(2)}) collective-permute-start(bf16[20,2,32,256]{3,2,1,0:T(8,128)(2,1)S(1)} %get-tuple-element.333), channel_id=1, source_target_pairs={{0,1},{1,2},{2,3},{3,4},{4,5},{5,6},{6,7},{7,8},{8,9},{9,10},{10,1... | collective-permute-start | bytes 1966088 | tf_op jit(solution)/shard_map/ppermute | solution.py:24
  177.4 132.1 %collective-permute-start.4 = (bf16[2,8,2048]{2,1,0:T(8,128)(2,1)}, bf16[2,8,2048]{2,1,0:T(8,128)(2,1)}, u32[]{:S(2)}, u32[]{:S(2)}) collective-permute-start(bf16[2,8,2048]{2,1,0:T(8,128)(2,1)} %slice.5004), channel_id=1, source_target_pairs={{0,16},{16,32},{32,48},{48,64},{64,80},{80,96},{96,112},{1,17},{17... | collective-permute-start | bytes 196616 | tf_op jit(solution)/shard_map/ppermute | solution.py:24
  185.6 104.9 %collective-permute-start.12 = (bf16[2,2,2048]{2,1,0:T(2,128)(2,1)}, bf16[2,2,2048]{2,1,0:T(2,128)(2,1)}, u32[]{:S(2)}, u32[]{:S(2)}) collective-permute-start(bf16[2,2,2048]{2,1,0:T(2,128)(2,1)} %reshape.1634), channel_id=1, source_target_pairs={{0,16},{16,32},{32,48},{48,64},{64,80},{80,96},{96,112},{1,17},{17... | collective-permute-start | bytes 49160 | tf_op jit(solution)/shard_map/ppermute | solution.py:24
  190.4 93.6 %all-to-all-start = ((bf16[4,2,1024]{2,1,0:T(2,128)(2,1)}), bf16[4,2,1024]{2,1,0:T(2,128)(2,1)S(1)}, u32[]{:S(2)}, u32[]{:S(2)}) async-start(bf16[4,2,1024]{2,1,0:T(2,128)(2,1)} %reshape.2124), calls=%async_computation | async-start | bytes 32768 | tf_op jit(solution)/shard_map/all_to_all | solution.py:15
  198.9 97.5 %collective-permute-start.8 = (bf16[2,4,2048]{2,1,0:T(4,128)(2,1)}, bf16[2,4,2048]{2,1,0:T(4,128)(2,1)}, u32[]{:S(2)}, u32[]{:S(2)}) collective-permute-start(bf16[2,4,2048]{2,1,0:T(4,128)(2,1)} %slice.5302), channel_id=1, source_target_pairs={{0,16},{16,32},{32,48},{48,64},{64,80},{80,96},{96,112},{1,17},{17... | collective-permute-start | bytes 98312 | tf_op jit(solution)/shard_map/ppermute | solution.py:24
  278.0 16.4 %collective-permute-start.13 = (bf16[2,2,2048]{2,1,0:T(2,128)(2,1)}, bf16[2,2,2048]{2,1,0:T(2,128)(2,1)S(1)}, u32[]{:S(2)}, u32[]{:S(2)}) collective-permute-start(bf16[2,2,2048]{2,1,0:T(2,128)(2,1)} %reshape.1634), channel_id=1, source_target_pairs={{16,0},{32,16},{48,32},{64,48},{80,64},{96,80},{112,96},{17,1},{33... | collective-permute-start | bytes 49160 | tf_op jit(solution)/shard_map/ppermute | solution.py:27
  281.9 33.9 %collective-permute-start.5 = (bf16[2,8,2048]{2,1,0:T(8,128)(2,1)S(1)}, bf16[2,8,2048]{2,1,0:T(8,128)(2,1)S(1)}, u32[]{:S(2)}, u32[]{:S(2)}) collective-permute-start(bf16[2,8,2048]{2,1,0:T(8,128)(2,1)S(1)} %slice.5006), channel_id=1, source_target_pairs={{16,0},{32,16},{48,32},{64,48},{80,64},{96,80},{112,96},{17,1},{33... | collective-permute-start | bytes 196616 | tf_op jit(solution)/shard_map/ppermute | solution.py:27
  284.8 18.5 %all-to-all-start.1 = ((bf16[4,4,1,2048]{3,1,2,0:T(4,128)(2,1)}), bf16[4,4,1,2048]{3,1,2,0:T(4,128)(2,1)S(1)}, u32[]{:S(2)}, u32[]{:S(2)}) async-start(bf16[4,4,1,2048]{3,1,2,0:T(4,128)(2,1)} %stack.157), calls=%async_computation.1 | async-start | bytes 131072 | tf_op jit(solution)/shard_map/all_to_all | solution.py:15
  290.5 10.6 %collective-permute-start.9 = (bf16[2,4,2048]{2,1,0:T(4,128)(2,1)S(1)}, bf16[2,4,2048]{2,1,0:T(4,128)(2,1)S(1)}, u32[]{:S(2)}, u32[]{:S(2)}) collective-permute-start(bf16[2,4,2048]{2,1,0:T(4,128)(2,1)S(1)} %slice.5304), channel_id=1, source_target_pairs={{16,0},{32,16},{48,32},{64,48},{80,64},{96,80},{112,96},{17,1},{33... | collective-permute-start | bytes 98312 | tf_op jit(solution)/shard_map/ppermute | solution.py:27
  294.4 24.2 %collective-permute-start.15 = (bf16[6,2,2048]{2,1,0:T(2,128)(2,1)S(1)}, bf16[6,2,2048]{2,1,0:T(2,128)(2,1)S(1)}, u32[]{:S(2)}, u32[]{:S(2)}) collective-permute-start(bf16[6,2,2048]{2,1,0:T(2,128)(2,1)S(1)} %constant_dynamic-update-slice_fusion.9), channel_id=1, source_target_pairs={{1,0},{2,1},{3,2},{4,3},{5,4},{6,5},{7,6},{8,7},{9,8},{10,9},{11,1... | collective-permute-start | bytes 147464 | tf_op jit(solution)/shard_map/ppermute | solution.py:27
  296.4 28.5 %collective-permute-start.14 = (bf16[6,2,2048]{2,1,0:T(2,128)(2,1)S(1)}, bf16[6,2,2048]{2,1,0:T(2,128)(2,1)S(1)}, u32[]{:S(2)}, u32[]{:S(2)}) collective-permute-start(bf16[6,2,2048]{2,1,0:T(2,128)(2,1)S(1)} %constant_dynamic-update-slice_fusion.9), channel_id=1, source_target_pairs={{0,1},{1,2},{2,3},{3,4},{4,5},{5,6},{6,7},{7,8},{8,9},{9,10},{10,1... | collective-permute-start | bytes 147464 | tf_op jit(solution)/shard_map/ppermute | solution.py:24
  301.3 98.1 %collective-permute-start.10 = (bf16[8,2,2048]{2,1,0:T(2,128)(2,1)S(1)}, bf16[8,2,2048]{2,1,0:T(2,128)(2,1)S(1)}, u32[]{:S(2)}, u32[]{:S(2)}) collective-permute-start(bf16[8,2,2048]{2,1,0:T(2,128)(2,1)S(1)} %get-tuple-element.509), channel_id=1, source_target_pairs={{0,1},{1,2},{2,3},{3,4},{4,5},{5,6},{6,7},{7,8},{8,9},{9,10},{10,1... | collective-permute-start | bytes 196616 | tf_op jit(solution)/shard_map/ppermute | solution.py:24
  304.0 132.8 %all-to-all-start.2 = ((bf16[4,16,1,2048]{3,1,2,0:T(8,128)(2,1)}), bf16[4,16,1,2048]{3,1,2,0:T(8,128)(2,1)S(1)}, u32[]{:S(2)}, u32[]{:S(2)}) async-start(bf16[4,16,1,2048]{3,1,2,0:T(8,128)(2,1)} %stack.158), calls=%async_computation.2 | async-start | bytes 524288 | tf_op jit(solution)/shard_map/all_to_all | solution.py:15
  309.5 89.9 %collective-permute-start.11 = (bf16[8,2,2048]{2,1,0:T(2,128)(2,1)S(1)}, bf16[8,2,2048]{2,1,0:T(2,128)(2,1)S(1)}, u32[]{:S(2)}, u32[]{:S(2)}) collective-permute-start(bf16[8,2,2048]{2,1,0:T(2,128)(2,1)S(1)} %get-tuple-element.510), channel_id=1, source_target_pairs={{1,0},{2,1},{3,2},{4,3},{5,4},{6,5},{7,6},{8,7},{9,8},{10,9},{11,1... | collective-permute-start | bytes 196616 | tf_op jit(solution)/shard_map/ppermute | solution.py:27
  316.6 96.0 %collective-permute-start.6 = (bf16[12,2,2048]{2,1,0:T(2,128)(2,1)}, bf16[12,2,2048]{2,1,0:T(2,128)(2,1)}, u32[]{:S(2)}, u32[]{:S(2)}) collective-permute-start(bf16[12,2,2048]{2,1,0:T(2,128)(2,1)} %get-tuple-element.503), channel_id=1, source_target_pairs={{0,1},{1,2},{2,3},{3,4},{4,5},{5,6},{6,7},{7,8},{8,9},{9,10},{10,1... | collective-permute-start | bytes 294920 | tf_op jit(solution)/shard_map/ppermute | solution.py:24
  318.6 94.0 %collective-permute-start.7 = (bf16[12,2,2048]{2,1,0:T(2,128)(2,1)}, bf16[12,2,2048]{2,1,0:T(2,128)(2,1)}, u32[]{:S(2)}, u32[]{:S(2)}) collective-permute-start(bf16[12,2,2048]{2,1,0:T(2,128)(2,1)} %get-tuple-element.504), channel_id=1, source_target_pairs={{1,0},{2,1},{3,2},{4,3},{5,4},{6,5},{7,6},{8,7},{9,8},{10,9},{11,1... | collective-permute-start | bytes 294920 | tf_op jit(solution)/shard_map/ppermute | solution.py:27
  330.2 70.0 %copy-start.41 = (bf16[64,64]{0,1:T(8,128)(2,1)S(1)}, bf16[64,64]{0,1:T(8,128)(2,1)}, u32[]{:S(2)}) copy-start(bf16[64,64]{0,1:T(8,128)(2,1)} %get-tuple-element.414) | copy-start | bytes 24580
  330.2 70.0 %copy-start.42 = (bf16[64,64]{0,1:T(8,128)(2,1)S(1)}, bf16[64,64]{0,1:T(8,128)(2,1)}, u32[]{:S(2)}) copy-start(bf16[64,64]{0,1:T(8,128)(2,1)} %get-tuple-element.416) | copy-start | bytes 24580
  330.4 70.1 %copy-start.43 = (bf16[64,64]{0,1:T(8,128)(2,1)S(1)}, bf16[64,64]{0,1:T(8,128)(2,1)}, u32[]{:S(2)}) copy-start(bf16[64,64]{0,1:T(8,128)(2,1)} %get-tuple-element.418) | copy-start | bytes 24580
  330.4 70.3 %copy-start.45 = (bf16[64,64]{0,1:T(8,128)(2,1)S(1)}, bf16[64,64]{0,1:T(8,128)(2,1)}, u32[]{:S(2)}) copy-start(bf16[64,64]{0,1:T(8,128)(2,1)} %get-tuple-element.404) | copy-start | bytes 24580
  330.4 70.3 %copy-start.47 = (bf16[64,64]{0,1:T(8,128)(2,1)S(1)}, bf16[64,64]{0,1:T(8,128)(2,1)}, u32[]{:S(2)}) copy-start(bf16[64,64]{0,1:T(8,128)(2,1)} %get-tuple-element.399) | copy-start | bytes 24580
  330.5 70.3 %copy-start.44 = (bf16[64,64]{0,1:T(8,128)(2,1)S(1)}, bf16[64,64]{0,1:T(8,128)(2,1)}, u32[]{:S(2)}) copy-start(bf16[64,64]{0,1:T(8,128)(2,1)} %get-tuple-element.408) | copy-start | bytes 24580
  330.5 70.5 %copy-start.49 = (bf16[64,64]{0,1:T(8,128)(2,1)S(1)}, bf16[64,64]{0,1:T(8,128)(2,1)}, u32[]{:S(2)}) copy-start(bf16[64,64]{0,1:T(8,128)(2,1)} %get-tuple-element.392) | copy-start | bytes 24580
  330.5 70.6 %copy-start.50 = (bf16[64,64]{0,1:T(8,128)(2,1)S(1)}, bf16[64,64]{0,1:T(8,128)(2,1)}, u32[]{:S(2)}) copy-start(bf16[64,64]{0,1:T(8,128)(2,1)} %get-tuple-element.391) | copy-start | bytes 24580
  330.5 70.7 %copy-start.48 = (bf16[64,64]{0,1:T(8,128)(2,1)S(1)}, bf16[64,64]{0,1:T(8,128)(2,1)}, u32[]{:S(2)}) copy-start(bf16[64,64]{0,1:T(8,128)(2,1)} %get-tuple-element.393) | copy-start | bytes 24580
  347.0 54.7 %copy-start.39 = (bf16[64,64]{0,1:T(8,128)(2,1)S(1)}, bf16[64,64]{0,1:T(8,128)(2,1)}, u32[]{:S(2)}) copy-start(bf16[64,64]{0,1:T(8,128)(2,1)} %get-tuple-element.406) | copy-start | bytes 24580
  347.0 55.1 %copy-start.96 = (bf16[64,64]{0,1:T(8,128)(2,1)S(1)}, bf16[64,64]{0,1:T(8,128)(2,1)}, u32[]{:S(2)}) copy-start(bf16[64,64]{0,1:T(8,128)(2,1)} %get-tuple-element.383) | copy-start | bytes 24580
  347.1 55.1 %copy-start.102 = (bf16[64,64]{0,1:T(8,128)(2,1)S(1)}, bf16[64,64]{0,1:T(8,128)(2,1)}, u32[]{:S(2)}) copy-start(bf16[64,64]{0,1:T(8,128)(2,1)} %get-tuple-element.384) | copy-start | bytes 24580
  (341 other events, 2861.2 us)
